TPU v7x, 32 devices: a whole 2x2x4 slice. The times are simulated.
32 devices in a mesh: node: 16 (over z, y, core), ell: 2 (over x).
Axes of the slice: x: 2, y: 2, z: 4, core: 2. Of those that a mesh axis runs over, the one named last changes fastest.
Arguments:
- table_zero: bfloat16 [6144, 1536], P('node', 'ell'), may hold values from -1 to 1
- table_two: bfloat16 [6144, 1536], P('node', 'ell'), may hold values from -1 to 1
- spectrum: bfloat16 [1536], P('ell'), may hold values from -0.15625 to 0.15625
- weights: float32 [6144], P('node'), may hold values from 0.02551552 to 0.25515518
Outputs:
- kernel: float32 [1536, 1536], P('node', 'ell')
All inputs are finite; a program needn't handle non-finite values.
Results may differ from a plain program's by a relative error of at most 0.0029.
Values may be sent and summed in bfloat16 or wider, within the bound.
A program may use at most 128 MiB of HBM per device.

v0:
```python
import jax
import jax.numpy as jnp
from jax import lax
from jax.sharding import PartitionSpec as P


def contract_nodes(left, right):
    return lax.dot_general(
        left, right, (((0,), (0,)), ((), ())), preferred_element_type=jnp.float32
    )


def per_device(table_zero, table_two, spectrum, weights):
    partial_value = jnp.dot(table_zero, spectrum, preferred_element_type=jnp.float32)
    xi = lax.psum(partial_value, "ell")
    gathered = lax.all_gather(table_zero, "ell", axis=1, tiled=True)
    weighted = ((weights * xi)[:, None] * gathered.astype(jnp.float32)).astype(jnp.bfloat16)
    return lax.psum_scatter(
        contract_nodes(weighted, table_two), "node", scatter_dimension=0, tiled=True
    )


def solution(mesh):
    placed = (P("node", "ell"), P("node", "ell"), P("ell"), P("node"))
    return jax.shard_map(
        per_device, mesh=mesh, in_specs=placed, out_specs=P("node", "ell"), check_vma=False
    )
```

profile of v0, /device:TPU:0, one launch (start us, length us, event | category | flops | bytes accessed | tf_op | source)
XLA Modules:
  0.0 121.9 jit_solution(10760141810804105223)
XLA Ops:
  6.5 0.0 copy-start
  6.5 0.0 all-gather.2.cloned.1.call-start
  6.5 0.7 all-gather.2.cloned.1.call-update
  7.3 0.0 reduce-scatter.2.cloned.1.call-start
  7.3 0.7 reshape.1
  8.0 1.4 %convolution_reduce_fusion = f32[384]{0:T(512)S(1)} fusion(bf16[384,768]{1,0:T(8,128)(2,1)} %param.4, bf16[768,1]{0,1:T(2,128)(2,1)S(1)} %reshape.1), kind=kOutput, calls=%fused_computation.3 | convolution fusion | flops 589824 | bytes 592896 | tf_op jit(solution)/shard_map/dot_general | solution.py:14
  9.3 5.8 %psum.7 = f32[384]{0:T(512)S(1)} all-reduce(f32[384]{0:T(512)S(1)} %convolution_reduce_fusion), channel_id=1, replica_groups=mesh['node'=16,'ell'=2] {'ell'}, use_global_device_ids=true, to_apply=%region_0.0 | all-reduce | flops 384 | bytes 3072 | tf_op jit(solution)/shard_map/psum | solution.py:15
  15.2 0.7 mul.11
  15.9 18.5 %all-gather.2.cloned.1.call-done = bf16[384,1536]{1,0:T(8,128)(2,1)} async-done(((bf16[384,768]{1,0:T(8,128)(2,1)}), bf16[384,1536]{1,0:T(8,128)(2,1)}) %all-gather.2.cloned.1.call-update) | async-done | bytes 1179664 | tf_op jit(solution)/shard_map/all_gather | solution.py:16
  34.4 0.0 copy-done
  34.4 4.9 %fusion = f32[1536,768]{1,0:T(8,128)} fusion(bf16[384,768]{1,0:T(8,128)(2,1)S(1)} %copy-done, bf16[384,1536]{1,0:T(8,128)(2,1)} %all-gather.2.cloned.1.call-done, f32[384]{0:T(512)S(1)} %mul.11), kind=kOutput, calls=%fused_computation.1 | convolution fusion | flops 907739136 | bytes 6489600 | tf_op jit(solution)/shard_map/dot_general | solution.py:8
  39.3 0.0 reduce-scatter.2.cloned.1.call-update
  39.3 75.7 %reduce-scatter.2.cloned.1.call-done = f32[96,768]{1,0:T(8,128)} async-done(((f32[1536,768]{1,0:T(8,128)}), f32[96,768]{1,0:T(8,128)}) %reduce-scatter.2.cloned.1.call-update) | async-done | bytes 294928 | tf_op jit(solution)/shard_map/reduce_scatter | solution.py:18
Async XLA Ops:
  6.5 27.9 %copy-start = (bf16[384,768]{1,0:T(8,128)(2,1)S(1)}, bf16[384,768]{1,0:T(8,128)(2,1)}, u32[]{:S(2)}) copy-start(bf16[384,768]{1,0:T(8,128)(2,1)} %param.5) | copy-start | bytes 1769476
  6.5 27.8 %all-gather.2.cloned.1.call-start = ((), (), s32[]{:S(2)}) async-start(), calls=%async_computation.1 | async-start | bytes 1769472 | tf_op jit(solution)/shard_map/all_gather | solution.py:16
  7.3 107.8 %reduce-scatter.2.cloned.1.call-start = ((), (), s32[]{:S(2)}) async-start(), calls=%async_computation.2 | async-start | bytes 5013504 | tf_op jit(solution)/shard_map/reduce_scatter | solution.py:18
Sparse Core Ops, SparseCore 0:
  8.9 25.4 all-gather.1
  39.4 75.5 reduce-scatter.1
where the time goes:
time: 122 us
  waiting for transfers between devices  94.9 us (78%)
  between operations  13.4 us (11%)
  matrix products  6.26 us (5%)
  blocking collectives  5.85 us (5%)
    reduce_scatter x1, waiting for transfers between devices, per_device(): lax.psum_scatter(contract_nodes(weighted, table_two), 'node', scatter_dim...  75.7 us
    all_gather x1, waiting for transfers between devices, per_device(): gathered = lax.all_gather(table_zero, 'ell', axis=1, tiled=True)  18.5 us
    psum x1, blocking collectives, per_device(): xi = lax.psum(partial_value, 'ell')  5.85 us
    dot_general x1, matrix products, contract_nodes(): lax.dot_general(left, right, (((0,), (0,)), ((), ())), preferred_element_...  4.9 us
  transfers between devices with their start and end apart: 2, of which 2 were waited for; matrix products, arithmetic and copies ran while one was open for 2% of the time, Pallas kernels for 0%

commit v1 on v0

v1 whole, which is shorter than its diff:
```python
import functools

import jax
import jax.numpy as jnp
from jax import lax
from jax.experimental import pallas as pl
from jax.experimental.pallas import tpu as pltpu
from jax.sharding import PartitionSpec as P

MESH = pl.DeviceIdType.MESH
F32, BF16 = jnp.float32, jnp.bfloat16
SPLIT = 2


def kernel(nodes, ells, rows, tz, t2, spec, wts, out, gath, xsnd, xrcv, part, cbuf,
           ysnd, yrcv, zsnd, zrcv, g_s, g_r, x_s, x_r, c_s, c_r, y_s, y_r, z_s, z_r):
    depth, half = tz.shape
    zs_all, wide = nodes // 4, 4 * rows
    per = half // wide
    cols = t2.shape[1] // SPLIT
    n, e = lax.axis_index("node"), lax.axis_index("ell")
    c, y, z = lax.rem(n, 2), lax.rem(n // 2, 2), n // 4

    def at(zz, yy, cc):
        return (zz * 4 + yy * 2 + cc, e)

    def peer(d):
        return lax.rem(e + d, ells)

    def order(i, src):
        return jnp.where(src < ells // 2, i, per - 1 - i)

    barrier = pltpu.get_barrier_semaphore()
    greet = [(n, peer(d)) for d in range(1, ells)]
    greet += [at(z, y, 1 - c), at(z, 1 - y, c)]
    greet += [at(lax.rem(z + d, zs_all), y, c) for d in range(1, zs_all)]
    for device in greet:
        pl.semaphore_signal(barrier, inc=1, device_id=device, device_id_type=MESH)

    xsnd[...] = lax.dot_general(
        jnp.broadcast_to(spec[...], (16, half)), tz[...], (((1,), (1,)), ((), ())),
        preferred_element_type=F32)[:8]
    pl.semaphore_wait(barrier, len(greet))

    def remote(src, dst, s_sem, r_sem, device):
        return pltpu.make_async_remote_copy(
            src_ref=src, dst_ref=dst, send_sem=s_sem, recv_sem=r_sem,
            device_id=device, device_id_type=MESH)

    xi_copies, g_copies = [], {}
    for d in range(1, ells):
        xi_copies.append(remote(xsnd, xrcv.at[d - 1], x_s.at[d - 1], x_r.at[d - 1], (n, peer(d))))
        xi_copies[-1].start()
    for i in range(per):
        for d in range(1, ells):
            start = pl.multiple_of(order(i, e) * wide, 128)
            g_copies[d, i] = remote(
                tz.at[:, pl.ds(start, wide)], gath.at[d - 1, i],
                g_s.at[d - 1, i], g_r.at[d - 1, i], (n, peer(d)))
            g_copies[d, i].start()

    xi = xsnd[...]
    for d in range(1, ells):
        xi_copies[d - 1].wait_recv()
        xi = xi + xrcv[d - 1]
    scale = jnp.transpose(xi * wts[...])[:, 0:1]

    c_copies, y_copies, goal = {}, {}, {}

    def multiply(j):
        d, i = j // per, j % per
        src = lax.rem(e + ells - d, ells)
        goal[j] = src * per + order(i, src)
        if d == 0:
            raw = tz[:, pl.ds(pl.multiple_of(order(i, e) * wide, 128), wide)]
        else:
            g_copies[d, i].wait_recv()
            raw = gath[d - 1, i]
        weighted = (scale * raw.astype(F32)).astype(BF16)
        for s in range(SPLIT):
            prod = lax.dot_general(
                weighted, t2[:, s * cols:(s + 1) * cols], (((0,), (0,)), ((), ())),
                preferred_element_type=F32)
            for cc in range(2):
                for yy in range(2):
                    k = (2 * yy + cc) * rows
                    part[j, s, cc, yy] = prod[k:k + rows]
            c_copies[j, s] = remote(
                part.at[j, s, 1 - c], cbuf.at[j, s], c_s.at[j, s], c_r.at[j, s],
                at(z, y, 1 - c))
            c_copies[j, s].start()

    def over_y(j):
        for s in range(SPLIT):
            c_copies[j, s].wait_recv()
            ysnd[j, s] = (part[j, s, c, 1 - y] + cbuf[j, s, 1 - y]).astype(BF16)
            y_copies[j, s] = remote(
                ysnd.at[j, s], yrcv.at[j, s], y_s.at[j, s], y_r.at[j, s], at(z, 1 - y, c))
            y_copies[j, s].start()

    def z_copy(j, s):
        return remote(zsnd.at[j, s], zrcv.at[z, s], z_s.at[j, s], z_r.at[z, s], at(goal[j], y, c))

    def over_z(j):
        for s in range(SPLIT):
            y_copies[j, s].wait_recv()
            total = part[j, s, c, y] + cbuf[j, s, y] + yrcv[j, s].astype(F32)

            @pl.when(goal[j] == z)
            def _():
                out[:, s * cols:(s + 1) * cols] = total

            @pl.when(goal[j] != z)
            def _():
                zsnd[j, s] = total.astype(BF16)
                z_copy(j, s).start()

    for j in range(per):
        multiply(j)
    for j in range(per):
        over_y(j)
    pending = list(range(per))
    for j in range(per, zs_all):
        multiply(j)
        over_y(j)
        for k in pending:
            over_z(k)
        pending = [j]
    for k in pending:
        over_z(k)

    for s in range(SPLIT):
        for k in range(zs_all):
            @pl.when(k != z)
            def _():
                remote(zsnd.at[0, s], zrcv.at[k, s], z_s.at[0, s], z_r.at[k, s], at(k, y, c)).wait_recv()
                out[:, s * cols:(s + 1) * cols] += zrcv[k, s].astype(F32)

    for copy in xi_copies + list(g_copies.values()) + list(c_copies.values()) + list(y_copies.values()):
        copy.wait_send()
    for j in range(zs_all):
        for s in range(SPLIT):
            @pl.when(goal[j] != z)
            def _():
                z_copy(j, s).wait_send()


def per_device(nodes, ells, table_zero, table_two, spectrum, weights):
    depth, half = table_zero.shape
    rows = half * ells // nodes
    width = table_two.shape[1]
    zs_all, per, cols = nodes // 4, half // (4 * rows), width // SPLIT
    peers = max(ells - 1, 1)
    dma = pltpu.SemaphoreType.DMA
    vmem = pl.BlockSpec(memory_space=pltpu.VMEM)
    return pl.pallas_call(
        functools.partial(kernel, nodes, ells, rows),
        out_shape=jax.ShapeDtypeStruct((rows, width), F32),
        in_specs=[vmem] * 4,
        out_specs=vmem,
        scratch_shapes=[
            pltpu.VMEM((peers, per, depth, 4 * rows), BF16),
            pltpu.VMEM((8, depth), F32),
            pltpu.VMEM((peers, 8, depth), F32),
            pltpu.VMEM((zs_all, SPLIT, 2, 2, rows, cols), F32),
            pltpu.VMEM((zs_all, SPLIT, 2, rows, cols), F32),
            pltpu.VMEM((zs_all, SPLIT, rows, cols), BF16),
            pltpu.VMEM((zs_all, SPLIT, rows, cols), BF16),
            pltpu.VMEM((zs_all, SPLIT, rows, cols), BF16),
            pltpu.VMEM((zs_all, SPLIT, rows, cols), BF16),
            dma((peers, per)), dma((peers, per)),
            dma((peers,)), dma((peers,)),
            dma((zs_all, SPLIT)), dma((zs_all, SPLIT)),
            dma((zs_all, SPLIT)), dma((zs_all, SPLIT)),
            dma((zs_all, SPLIT)), dma((zs_all, SPLIT)),
        ],
        compiler_params=pltpu.CompilerParams(
            collective_id=0, has_side_effects=True, vmem_limit_bytes=60 * 1024 * 1024),
    )(table_zero, table_two, spectrum.reshape(1, half), weights.reshape(1, depth))


def solution(mesh):
    placed = (P("node", "ell"), P("node", "ell"), P("ell"), P("node"))
    return jax.shard_map(
        functools.partial(per_device, mesh.shape["node"], mesh.shape["ell"]),
        mesh=mesh, in_specs=placed, out_specs=P("node", "ell"), check_vma=False)
```

time: 122 us -> 39.7 us (0.33)
  the two profiles are of different devices: /device:TPU:0 before, /device:TPU:17 now
where the time goes in v1:
time: 39.7 us; the launch traced here: 39.5 us
  Pallas kernels  35.9 us (90%)
  local copies, waits for them, and re-layouts  3.56 us (9%)
    pallas_call x1, Pallas kernels, per_device(): pl.pallas_call(functools.partial(kernel, nodes, ells, rows), out_shape=ja...  35.9 us
    unnamed x3, local copies, waits for them, and re-layouts  1.7 us
    reshape x1, local copies, waits for them, and re-layouts, per_device(): weights.reshape(1, depth)  1.28 us

profile of v1, /device:TPU:17, one launch (start us, length us, event | category | flops | bytes accessed | tf_op | source)
XLA Modules:
  0.0 39.5 jit_solution(17467516451357639315)
XLA Ops:
  0.0 0.0 copy-start
  0.0 1.3 %reshape.7.wts = f32[1,384]{1,0:T(1,128)} reshape(f32[384]{0:T(512)} %param.7) | data formatting | bytes 3072 | tf_op jit(solution)/shard_map/reshape | solution.py:179
  1.3 0.0 copy-done
  1.3 0.6 %reshape.6.spec = bf16[1,768]{1,0:T(2,128)(2,1)} reshape(bf16[768]{0:T(1024)(128)(2,1)S(1)} %copy-done) | data formatting | bytes 3072 | tf_op jit(solution)/shard_map/reshape | solution.py:179
  1.9 35.9 %shard_map.46 = f32[96,768]{1,0:T(8,128)} custom-call(bf16[384,768]{1,0:T(8,128)(2,1)} %tz.1, bf16[384,768]{1,0:T(8,128)(2,1)} %t2.1, bf16[1,768]{1,0:T(2,128)(2,1)} %reshape.6.spec, f32[1,384]{1,0:T(1,128)} %reshape.7.wts), custom_call_target="tpu_custom_call" | custom-call | tf_op jit(solution)/shard_map/pallas_call | solution.py:156
  37.8 1.7 %copy.6 = f32[96,768]{1,0:T(8,128)} copy(f32[96,768]{1,0:T(8,128)} %shard_map.46) | data formatting | bytes 589824
Async XLA Ops:
  0.0 1.3 %copy-start = (bf16[768]{0:T(1024)(128)(2,1)S(1)}, bf16[768]{0:T(1024)(128)(2,1)}, u32[]{:S(2)}) copy-start(bf16[768]{0:T(1024)(128)(2,1)} %param.6) | copy-start | bytes 4612

commit v2 on v0

v2 whole, which is shorter than its diff:
```python
import functools

import jax
import jax.numpy as jnp
from jax import lax
from jax.experimental import pallas as pl
from jax.experimental.pallas import tpu as pltpu
from jax.sharding import PartitionSpec as P

MESH = pl.DeviceIdType.MESH
F32, BF16 = jnp.float32, jnp.bfloat16
PARTS = 3


def kernel(nodes, ells, rows, tz_hbm, t2_hbm, spec, wts, out, tz, t2, own, gath, xsnd, xrcv,
           part, cbuf, ysnd, yrcv, zsnd, zrcv, in_s, g_s, g_r, x_s, x_r, c_s, c_r,
           y_s, y_r, z_s, z_r):
    depth, half = tz.shape
    zs_all, wide, sub = nodes // 4, 4 * rows, rows // PARTS
    slabs = half // wide
    per = slabs * PARTS
    n, e = lax.axis_index("node"), lax.axis_index("ell")
    c, y, z = lax.rem(n, 2), lax.rem(n // 2, 2), n // 4

    def at(zz, yy, cc):
        return (zz * 4 + yy * 2 + cc, e)

    def peer(d):
        return lax.rem(e + d, ells)

    def order(q, src):
        return jnp.where(src < ells // 2, q, slabs - 1 - q)

    loads = [pltpu.make_async_copy(tz_hbm, tz, in_s.at[0]),
             pltpu.make_async_copy(t2_hbm, t2, in_s.at[1])]
    for load in loads:
        load.start()
    barrier = pltpu.get_barrier_semaphore()
    greet = [(n, peer(d)) for d in range(1, ells)]
    greet += [at(z, y, 1 - c), at(z, 1 - y, c)]
    greet += [at(lax.rem(z + d, zs_all), y, c) for d in range(1, zs_all)]
    for device in greet:
        pl.semaphore_signal(barrier, inc=1, device_id=device, device_id_type=MESH)

    def remote(src, dst, s_sem, r_sem, device):
        return pltpu.make_async_remote_copy(
            src_ref=src, dst_ref=dst, send_sem=s_sem, recv_sem=r_sem,
            device_id=device, device_id_type=MESH)

    loads[0].wait()
    xsnd[...] = lax.dot_general(
        jnp.broadcast_to(spec[...].reshape(1, half), (16, half)), tz[...],
        (((1,), (1,)), ((), ())), preferred_element_type=F32)[:8]

    xi_copies, g_copies = [], {}
    for q in range(slabs):
        start = pl.multiple_of(order(q, e) * wide, 128)
        turned = jnp.transpose(tz[:, pl.ds(start, wide)])
        for t in range(PARTS):
            for k in range(4):
                low = k * rows + t * sub
                own[q * PARTS + t, k * sub:(k + 1) * sub] = turned[low:low + sub]
        if q == 0:
            pl.semaphore_wait(barrier, len(greet))
            for d in range(1, ells):
                xi_copies.append(remote(
                    xsnd, xrcv.at[d - 1], x_s.at[d - 1], x_r.at[d - 1], (n, peer(d))))
                xi_copies[-1].start()
        for i in range(q * PARTS, (q + 1) * PARTS):
            for d in range(1, ells):
                g_copies[d, i] = remote(
                    own.at[i], gath.at[d - 1, i], g_s.at[d - 1, i], g_r.at[d - 1, i],
                    (n, peer(d)))
                g_copies[d, i].start()

    xi = xsnd[...]
    for d in range(1, ells):
        xi_copies[d - 1].wait_recv()
        xi = xi + xrcv[d - 1]
    scale = xi[0:1] * wts[...].reshape(1, depth)
    loads[1].wait()

    c_copies, y_copies, goal = {}, {}, {}

    def multiply(j):
        d, i = j // per, j % per
        src = lax.rem(e + ells - d, ells)
        goal[j] = src * slabs + order(i // PARTS, src)
        if d == 0:
            raw = own[i]
        else:
            g_copies[d, i].wait_recv()
            raw = gath[d - 1, i]
        weighted = (scale * raw.astype(F32)).astype(BF16)
        prod = jnp.dot(weighted, t2[...], preferred_element_type=F32)
        for cc in range(2):
            for yy in range(2):
                k = (2 * yy + cc) * sub
                part[j, cc, yy] = prod[k:k + sub]
        c_copies[j] = remote(
            part.at[j, 1 - c], cbuf.at[j], c_s.at[j], c_r.at[j], at(z, y, 1 - c))
        c_copies[j].start()

    def over_y(j):
        c_copies[j].wait_recv()
        ysnd[j] = (part[j, c, 1 - y] + cbuf[j, 1 - y]).astype(BF16)
        y_copies[j] = remote(ysnd.at[j], yrcv.at[j], y_s.at[j], y_r.at[j], at(z, 1 - y, c))
        y_copies[j].start()

    def z_copy(j):
        t = j % PARTS
        return remote(zsnd.at[j], zrcv.at[z, t], z_s.at[j], z_r.at[z, t], at(goal[j], y, c))

    def over_z(j):
        t = j % PARTS
        y_copies[j].wait_recv()
        total = part[j, c, y] + cbuf[j, y] + yrcv[j].astype(F32)

        @pl.when(goal[j] == z)
        def _():
            out[t * sub:(t + 1) * sub] = total

        @pl.when(goal[j] != z)
        def _():
            zsnd[j] = total.astype(BF16)
            z_copy(j).start()

    count = zs_all * PARTS
    for j in range(per):
        multiply(j)
        if j:
            over_y(j - 1)
    over_y(per - 1)
    pending = list(range(per))
    for j in range(per, count):
        multiply(j)
        over_y(j)
        for _ in range(min(2, len(pending))):
            over_z(pending.pop(0))
        pending.append(j)
    for j in pending:
        over_z(j)

    for t in range(PARTS):
        for k in range(zs_all):
            @pl.when(k != z)
            def _():
                remote(zsnd.at[t], zrcv.at[k, t], z_s.at[t], z_r.at[k, t], at(k, y, c)).wait_recv()
                out[t * sub:(t + 1) * sub] += zrcv[k, t].astype(F32)

    for copy in xi_copies + list(g_copies.values()) + list(c_copies.values()) + list(y_copies.values()):
        copy.wait_send()
    for j in range(count):
        @pl.when(goal[j] != z)
        def _():
            z_copy(j).wait_send()


def per_device(nodes, ells, table_zero, table_two, spectrum, weights):
    depth, half = table_zero.shape
    rows = half * ells // nodes
    width = table_two.shape[1]
    slabs, sub, peers = half // (4 * rows), rows // PARTS, max(ells - 1, 1)
    per, count = slabs * PARTS, nodes // 4 * PARTS
    dma = pltpu.SemaphoreType.DMA
    vmem = pl.BlockSpec(memory_space=pltpu.VMEM)
    anywhere = pl.BlockSpec(memory_space=pl.ANY)
    return pl.pallas_call(
        functools.partial(kernel, nodes, ells, rows),
        out_shape=jax.ShapeDtypeStruct((rows, width), F32),
        in_specs=[anywhere, anywhere, vmem, vmem],
        out_specs=vmem,
        scratch_shapes=[
            pltpu.VMEM((depth, half), BF16),
            pltpu.VMEM((depth, width), BF16),
            pltpu.VMEM((per, 4 * sub, depth), BF16),
            pltpu.VMEM((peers, per, 4 * sub, depth), BF16),
            pltpu.VMEM((8, depth), F32),
            pltpu.VMEM((peers, 8, depth), F32),
            pltpu.VMEM((count, 2, 2, sub, width), F32),
            pltpu.VMEM((count, 2, sub, width), F32),
            pltpu.VMEM((count, sub, width), BF16),
            pltpu.VMEM((count, sub, width), BF16),
            pltpu.VMEM((count, sub, width), BF16),
            pltpu.VMEM((nodes // 4, PARTS, sub, width), BF16),
            dma((2,)),
            dma((peers, per)), dma((peers, per)),
            dma((peers,)), dma((peers,)),
            dma((count,)), dma((count,)),
            dma((count,)), dma((count,)),
            dma((count,)), dma((nodes // 4, PARTS)),
        ],
        compiler_params=pltpu.CompilerParams(
            collective_id=0, has_side_effects=True, vmem_limit_bytes=60 * 1024 * 1024),
    )(table_zero, table_two, spectrum, weights)


def solution(mesh):
    placed = (P("node", "ell"), P("node", "ell"), P("ell"), P("node"))
    return jax.shard_map(
        functools.partial(per_device, mesh.shape["node"], mesh.shape["ell"]),
        mesh=mesh, in_specs=placed, out_specs=P("node", "ell"), check_vma=False)
```

time: 122 us -> 36.3 us (0.30)
  the two profiles are of different devices: /device:TPU:0 before, /device:TPU:17 now
where the time goes in v2:
time: 36.3 us; the launch traced here: 36.1 us
  Pallas kernels  34.4 us (95%)
  local copies, waits for them, and re-layouts  1.69 us (5%)
    pallas_call x1, Pallas kernels, per_device(): pl.pallas_call(functools.partial(kernel, nodes, ells, rows), out_shape=ja...  34.4 us
    unnamed x1, local copies, waits for them, and re-layouts  1.69 us

profile of v2, /device:TPU:17, one launch (start us, length us, event | category | flops | bytes accessed | tf_op | source)
XLA Modules:
  0.0 36.1 jit_solution(1494151671757311484)
XLA Ops:
  0.0 34.4 %shard_map.46 = f32[96,768]{1,0:T(8,128)} custom-call(bf16[384,768]{1,0:T(8,128)(2,1)} %tz_hbm.1, bf16[384,768]{1,0:T(8,128)(2,1)} %t2_hbm.1, bf16[768]{0:T(1024)(128)(2,1)} %spec.1, f32[384]{0:T(512)} %wts.1), custom_call_target="tpu_custom_call" | custom-call | tf_op jit(solution)/shard_map/pallas_call | solution.py:168
  34.4 1.7 %copy.6 = f32[96,768]{1,0:T(8,128)} copy(f32[96,768]{1,0:T(8,128)} %shard_map.46) | data formatting | bytes 589824

commit v3 on v2

--- a/solution.py
+++ b/solution.py
@@ -128,17 +128,26 @@
     count = zs_all * PARTS
     for j in range(per):
         multiply(j)
-        if j:
-            over_y(j - 1)
-    over_y(per - 1)
-    pending = list(range(per))
+    sent, mine = [], list(range(per))
+
+    def next_y(j):
+        over_y(j)
+        sent.append(j)
+
+    for _ in range(min(2, per)):
+        next_y(mine.pop(0))
     for j in range(per, count):
         multiply(j)
-        over_y(j)
-        for _ in range(min(2, len(pending))):
-            over_z(pending.pop(0))
-        pending.append(j)
-    for j in pending:
+        if j > per + 1 and len(sent) > 1:
+            over_z(sent.pop(0))
+        next_y(j)
+        if mine:
+            next_y(mine.pop(0))
+        if j > per and len(sent) > 1:
+            over_z(sent.pop(0))
+    for j in mine:
+        next_y(j)
+    for j in sent:
         over_z(j)
 
     for t in range(PARTS):
@@ -167,7 +176,7 @@
     anywhere = pl.BlockSpec(memory_space=pl.ANY)
     return pl.pallas_call(
         functools.partial(kernel, nodes, ells, rows),
-        out_shape=jax.ShapeDtypeStruct((rows, width), F32),
+        out_shape=pltpu.VMEM((rows, width), F32),
         in_specs=[anywhere, anywhere, vmem, vmem],
         out_specs=vmem,
         scratch_shapes=[

time: 36.3 us -> 30.7 us (0.85)
  Pallas kernels: 34.4 us -> 29.8 us
  local copies, waits for them, and re-layouts: 1.69 us -> 0.72 us
    pallas_call x1, Pallas kernels: 34.4 us -> 29.8 us  [per_device(): pl.pallas_call(functools.partial(kernel, nodes, ells, rows), out_shape=pl...]
    unnamed x1, local copies, waits for them, and re-layouts: 1.69 us -> 0.72 us
where the time goes in v3:
time: 30.7 us; the launch traced here: 30.5 us
  Pallas kernels  29.8 us (97%)
  local copies, waits for them, and re-layouts  0.72 us (2%)
    pallas_call x1, Pallas kernels, per_device(): pl.pallas_call(functools.partial(kernel, nodes, ells, rows), out_shape=pl...  29.8 us
    unnamed x1, local copies, waits for them, and re-layouts  0.72 us

profile of v3, /device:TPU:17, one launch (start us, length us, event | category | flops | bytes accessed | tf_op | source)
XLA Modules:
  0.0 30.5 jit_solution(17183795551422948456)
XLA Ops:
  0.0 29.8 %shard_map.46 = f32[96,768]{1,0:T(8,128)S(1)} custom-call(bf16[384,768]{1,0:T(8,128)(2,1)} %tz_hbm.1, bf16[384,768]{1,0:T(8,128)(2,1)} %t2_hbm.1, bf16[768]{0:T(1024)(128)(2,1)} %spec.1, f32[384]{0:T(512)} %wts.1), custom_call_target="tpu_custom_call" | custom-call | tf_op jit(solution)/shard_map/pallas_call | solution.py:177
  29.8 0.7 %copy.6 = f32[96,768]{1,0:T(8,128)} copy(f32[96,768]{1,0:T(8,128)S(1)} %shard_map.46) | data formatting | bytes 589824

commit v4 on v3

--- a/solution.py
+++ b/solution.py
@@ -50,7 +50,7 @@
     loads[0].wait()
     xsnd[...] = lax.dot_general(
         jnp.broadcast_to(spec[...].reshape(1, half), (16, half)), tz[...],
-        (((1,), (1,)), ((), ())), preferred_element_type=F32)[:8]
+        (((1,), (1,)), ((), ())), preferred_element_type=F32)[:1]
 
     xi_copies, g_copies = [], {}
     for q in range(slabs):
@@ -134,7 +134,7 @@
         over_y(j)
         sent.append(j)
 
-    for _ in range(min(2, per)):
+    for _ in range(min(1, per)):
         next_y(mine.pop(0))
     for j in range(per, count):
         multiply(j)
@@ -184,8 +184,8 @@
             pltpu.VMEM((depth, width), BF16),
             pltpu.VMEM((per, 4 * sub, depth), BF16),
             pltpu.VMEM((peers, per, 4 * sub, depth), BF16),
-            pltpu.VMEM((8, depth), F32),
-            pltpu.VMEM((peers, 8, depth), F32),
+            pltpu.VMEM((1, depth), F32),
+            pltpu.VMEM((peers, 1, depth), F32),
             pltpu.VMEM((count, 2, 2, sub, width), F32),
             pltpu.VMEM((count, 2, sub, width), F32),
             pltpu.VMEM((count, sub, width), BF16),

time: 30.7 us -> 29.9 us (0.974)
  the two profiles are of different devices: /device:TPU:17 before, /device:TPU:0 now
where the time goes in v4:
time: 29.9 us; the launch traced here: 29.8 us
  Pallas kernels  29 us (97%)
  local copies, waits for them, and re-layouts  0.72 us (2%)
    pallas_call x1, Pallas kernels, per_device(): pl.pallas_call(functools.partial(kernel, nodes, ells, rows), out_shape=pl...  29 us
    unnamed x1, local copies, waits for them, and re-layouts  0.72 us

profile of v4, /device:TPU:0, one launch (start us, length us, event | category | flops | bytes accessed | tf_op | source)
XLA Modules:
  0.0 29.8 jit_solution(1876707396936603133)
XLA Ops:
  0.0 29.0 %shard_map.46 = f32[96,768]{1,0:T(8,128)S(1)} custom-call(bf16[384,768]{1,0:T(8,128)(2,1)} %tz_hbm.1, bf16[384,768]{1,0:T(8,128)(2,1)} %t2_hbm.1, bf16[768]{0:T(1024)(128)(2,1)} %spec.1, f32[384]{0:T(512)} %wts.1), custom_call_target="tpu_custom_call" | custom-call | tf_op jit(solution)/shard_map/pallas_call | solution.py:177
  29.0 0.7 %copy.6 = f32[96,768]{1,0:T(8,128)} copy(f32[96,768]{1,0:T(8,128)S(1)} %shard_map.46) | data formatting | bytes 589824
